TPU v7x, 32 devices: a whole 2x2x4 slice. The times are simulated.
32 devices in a mesh: tm: 32 (over z, y, x, core), chan: 1.
Axes of the slice: x: 2, y: 2, z: 4, core: 2. Of those that a mesh axis runs over, the one named last changes fastest.
Arguments:
- signal: bfloat16 [3, 4096, 512], P(None, 'tm', 'chan'), may hold values from -6 to 6
- taps: float32 [10, 2, 512], P(None, None, 'chan'), may hold values from -3 to 3
- w_gate: bfloat16 [10, 512, 2, 512], P(None, None, None, 'chan'), may hold values from -0.25 to 0.25
- w_res: bfloat16 [10, 512, 512], P(None, None, 'chan'), may hold values from -0.25 to 0.25
- w_skip: bfloat16 [10, 512, 512], P(None, None, 'chan'), may hold values from -0.1875 to 0.1875
Outputs:
- stream: bfloat16 [3, 4096, 512], P(None, 'tm', 'chan')
- skips: bfloat16 [3, 4096, 512], P(None, 'tm', 'chan')
All inputs are finite; a program needn't handle non-finite values.
Results may differ from a plain program's by a relative error of at most 0.02.
Values may be sent and summed in bfloat16 or wider, within the bound.
A program may use at most 64 MiB of HBM per device.

v0:
```python
import jax
import jax.numpy as jnp
from jax import lax
from jax.sharding import PartitionSpec as P

LAYERS = 10


def shifted(value, axis, steps):
    count = lax.axis_size(axis)
    leading, last = (max(0, -steps), min(count, count - steps))
    return lax.ppermute(value, axis, [(source, source + steps) for source in range(leading, last)])


def delay_block(stream, delay, near_fn, far_fn):
    length = stream.shape[1]
    whole, rest = divmod(delay, length)
    if whole == 0:
        nearer = stream
    else:
        nearer = near_fn(stream, whole)
    if rest == 0:
        return nearer
    farther = far_fn(stream[:, length - rest :], whole + 1)
    return jnp.concatenate([farther, nearer[:, : length - rest]], axis=1)


def near_time(block, steps):
    return shifted(block, "tm", steps)


def far_time(block, steps):
    return shifted(block, "tm", steps)


def gate_units(hidden):
    return (jnp.tanh(hidden[:, :, 0]) * jax.nn.sigmoid(hidden[:, :, 1])).astype(jnp.bfloat16)


def local(signal, taps, w_gate, w_res, w_skip):
    stream = signal
    seqs, length, local_c = stream.shape
    skip = jnp.zeros((seqs, length, local_c), jnp.float32)
    for layer in range(LAYERS):
        delayed = delay_block(stream, 2**layer, near_time, far_time)
        conv = (
            taps[layer, 0] * delayed.astype(jnp.float32)
            + taps[layer, 1] * stream.astype(jnp.float32)
        ).astype(jnp.bfloat16)
        gate_w = w_gate[layer]
        hidden = jnp.einsum(
            "stc,cko->stko",
            lax.all_gather(conv, "chan", axis=2, tiled=True),
            gate_w,
            preferred_element_type=jnp.float32,
        )
        gated = gate_units(hidden)
        res_w = w_res[layer]
        skip_w = w_skip[layer]
        piece = lax.all_gather(gated, "chan", axis=2, tiled=True)
        update = jnp.einsum("stc,co->sto", piece, res_w, preferred_element_type=jnp.float32)
        skip_part = jnp.einsum("stc,co->sto", piece, skip_w, preferred_element_type=jnp.float32)
        stream = (stream.astype(jnp.float32) + update).astype(jnp.bfloat16)
        skip = skip + skip_part
    return (stream, skip.astype(jnp.bfloat16))


def solution(mesh):
    in_specs = (
        P(None, "tm", "chan"),
        P(None, None, "chan"),
        P(None, None, None, "chan"),
        P(None, None, "chan"),
        P(None, None, "chan"),
    )
    out_specs = (P(None, "tm", "chan"), P(None, "tm", "chan"))
    return jax.shard_map(local, mesh=mesh, in_specs=in_specs, out_specs=out_specs, check_vma=False)
```

profile of v0, /device:TPU:8, one launch (start us, length us, event | category | flops | bytes accessed | tf_op | source)
XLA Modules:
  0.0 106.4 jit_solution(9999271078640858570)
XLA Ops:
  0.6 0.9 slice.253
  1.6 2.1 %collective-permute-start = (bf16[3,1,512]{2,1,0:T(2,128)(2,1)S(1)}, bf16[3,1,512]{2,1,0:T(2,128)(2,1)S(1)}, u32[]{:S(2)}, u32[]{:S(2)}) collective-permute-start(bf16[3,1,512]{2,1,0:T(2,128)(2,1)S(1)} %slice.253), channel_id=1, source_target_pairs={{0,1},{1,2},{2,3},{3,4},{4,5},{5,6},{6,7},{7,8},{8,9},{9,10},{10,1... | collective-permute-start | bytes 9224 | tf_op jit(solution)/shard_map/ppermute | solution.py:12
  3.6 10.4 %fusion.220 = (bf16[1,512,2,512]{3,2,1,0:T(2,128)(2,1)S(1)}, bf16[1,512,2,512]{3,2,1,0:T(2,128)(2,1)S(1)}, bf16[1,512,2,512]{3,2,1,0:T(2,128)(2,1)S(1)}, bf16[1,...) fusion(bf16[10,512,2,512]{3,2,1,0:T(2,128)(2,1)} %param.7), kind=kLoop, calls=%fused_computation.269 | loop fusion | bytes 20971520 | tf_op jit(solution)/shard_map/slice | solution.py:50
  15.5 3.5 %collective-permute-start.1 = (bf16[3,2,512]{2,1,0:T(2,128)(2,1)S(1)}, bf16[3,2,512]{2,1,0:T(2,128)(2,1)S(1)}, u32[]{:S(2)}, u32[]{:S(2)}) collective-permute-start(bf16[3,2,512]{2,1,0:T(2,128)(2,1)S(1)} %slice.338), channel_id=1, source_target_pairs={{0,1},{1,2},{2,3},{3,4},{4,5},{5,6},{6,7},{7,8},{8,9},{9,10},{10,1... | collective-permute-start | bytes 18440 | tf_op jit(solution)/shard_map/ppermute | solution.py:12
  19.0 3.2 %collective-permute-done.1 = bf16[3,2,512]{2,1,0:T(2,128)(2,1)S(1)} collective-permute-done((bf16[3,2,512]{2,1,0:T(2,128)(2,1)S(1)}, bf16[3,2,512]{2,1,0:T(2,128)(2,1)S(1)}, u32[]{:S(2)}, u32[]{:S(2)}) %collective-permute-start.1) | collective-permute-done | bytes 6176 | tf_op jit(solution)/shard_map/ppermute | solution.py:12
  23.6 1.9 %collective-permute-start.2 = (bf16[3,4,512]{2,1,0:T(4,128)(2,1)S(1)}, bf16[3,4,512]{2,1,0:T(4,128)(2,1)S(1)}, u32[]{:S(2)}, u32[]{:S(2)}) collective-permute-start(bf16[3,4,512]{2,1,0:T(4,128)(2,1)S(1)} %slice.342), channel_id=1, source_target_pairs={{0,1},{1,2},{2,3},{3,4},{4,5},{5,6},{6,7},{7,8},{8,9},{9,10},{10,1... | collective-permute-start | bytes 36872 | tf_op jit(solution)/shard_map/ppermute | solution.py:12
  25.5 4.9 %collective-permute-done.2 = bf16[3,4,512]{2,1,0:T(4,128)(2,1)S(1)} collective-permute-done((bf16[3,4,512]{2,1,0:T(4,128)(2,1)S(1)}, bf16[3,4,512]{2,1,0:T(4,128)(2,1)S(1)}, u32[]{:S(2)}, u32[]{:S(2)}) %collective-permute-start.2) | collective-permute-done | bytes 12320 | tf_op jit(solution)/shard_map/ppermute | solution.py:12
  30.4 0.6 fusion.18
  31.8 2.1 %collective-permute-start.3 = (bf16[3,8,512]{2,1,0:T(8,128)(2,1)S(1)}, bf16[3,8,512]{2,1,0:T(8,128)(2,1)S(1)}, u32[]{:S(2)}, u32[]{:S(2)}) collective-permute-start(bf16[3,8,512]{2,1,0:T(8,128)(2,1)S(1)} %slice.346), channel_id=1, source_target_pairs={{0,1},{1,2},{2,3},{3,4},{4,5},{5,6},{6,7},{7,8},{8,9},{9,10},{10,1... | collective-permute-start | bytes 73736 | tf_op jit(solution)/shard_map/ppermute | solution.py:12
  33.9 5.0 %collective-permute-done.3 = bf16[3,8,512]{2,1,0:T(8,128)(2,1)S(1)} collective-permute-done((bf16[3,8,512]{2,1,0:T(8,128)(2,1)S(1)}, bf16[3,8,512]{2,1,0:T(8,128)(2,1)S(1)}, u32[]{:S(2)}, u32[]{:S(2)}) %collective-permute-start.3) | collective-permute-done | bytes 24608 | tf_op jit(solution)/shard_map/ppermute | solution.py:12
  40.1 1.9 %collective-permute-start.4 = (bf16[3,16,512]{2,1,0:T(8,128)(2,1)S(1)}, bf16[3,16,512]{2,1,0:T(8,128)(2,1)S(1)}, u32[]{:S(2)}, u32[]{:S(2)}) collective-permute-start(bf16[3,16,512]{2,1,0:T(8,128)(2,1)S(1)} %slice.350), channel_id=1, source_target_pairs={{0,1},{1,2},{2,3},{3,4},{4,5},{5,6},{6,7},{7,8},{8,9},{9,10},{10,1... | collective-permute-start | bytes 147464 | tf_op jit(solution)/shard_map/ppermute | solution.py:12
  42.5 4.8 %collective-permute-done.4 = bf16[3,16,512]{2,1,0:T(8,128)(2,1)S(1)} collective-permute-done((bf16[3,16,512]{2,1,0:T(8,128)(2,1)S(1)}, bf16[3,16,512]{2,1,0:T(8,128)(2,1)S(1)}, u32[]{:S(2)}, u32[]{:S(2)}) %collective-permute-start.4) | collective-permute-done | bytes 49184 | tf_op jit(solution)/shard_map/ppermute | solution.py:12
  48.7 1.9 %collective-permute-start.5 = (bf16[3,32,512]{2,1,0:T(8,128)(2,1)S(1)}, bf16[3,32,512]{2,1,0:T(8,128)(2,1)S(1)}, u32[]{:S(2)}, u32[]{:S(2)}) collective-permute-start(bf16[3,32,512]{2,1,0:T(8,128)(2,1)S(1)} %slice.354), channel_id=1, source_target_pairs={{0,1},{1,2},{2,3},{3,4},{4,5},{5,6},{6,7},{7,8},{8,9},{9,10},{10,1... | collective-permute-start | bytes 294920 | tf_op jit(solution)/shard_map/ppermute | solution.py:12
  51.0 5.4 %collective-permute-done.5 = bf16[3,32,512]{2,1,0:T(8,128)(2,1)S(1)} collective-permute-done((bf16[3,32,512]{2,1,0:T(8,128)(2,1)S(1)}, bf16[3,32,512]{2,1,0:T(8,128)(2,1)S(1)}, u32[]{:S(2)}, u32[]{:S(2)}) %collective-permute-start.5) | collective-permute-done | bytes 98336 | tf_op jit(solution)/shard_map/ppermute | solution.py:12
  57.7 1.9 %collective-permute-start.6 = (bf16[3,64,512]{2,1,0:T(8,128)(2,1)S(1)}, bf16[3,64,512]{2,1,0:T(8,128)(2,1)S(1)}, u32[]{:S(2)}, u32[]{:S(2)}) collective-permute-start(bf16[3,64,512]{2,1,0:T(8,128)(2,1)S(1)} %get-tuple-element.12), channel_id=1, source_target_pairs={{0,1},{1,2},{2,3},{3,4},{4,5},{5,6},{6,7},{7,8},{8,9},{9,10},{10,1... | collective-permute-start | bytes 589832 | tf_op jit(solution)/shard_map/ppermute | solution.py:12
  60.0 6.5 %collective-permute-done.6 = bf16[3,64,512]{2,1,0:T(8,128)(2,1)S(1)} collective-permute-done((bf16[3,64,512]{2,1,0:T(8,128)(2,1)S(1)}, bf16[3,64,512]{2,1,0:T(8,128)(2,1)S(1)}, u32[]{:S(2)}, u32[]{:S(2)}) %collective-permute-start.6) | collective-permute-done | bytes 196640 | tf_op jit(solution)/shard_map/ppermute | solution.py:12
  67.8 1.9 %collective-permute-start.7 = (bf16[3,128,512]{2,1,0:T(8,128)(2,1)S(1)}, bf16[3,128,512]{2,1,0:T(8,128)(2,1)S(1)}, u32[]{:S(2)}, u32[]{:S(2)}) collective-permute-start(bf16[3,128,512]{2,1,0:T(8,128)(2,1)S(1)} %fusion.6), channel_id=1, source_target_pairs={{0,1},{1,2},{2,3},{3,4},{4,5},{5,6},{6,7},{7,8},{8,9},{9,10},{10,1... | collective-permute-start | bytes 1179656 | tf_op jit(solution)/shard_map/ppermute | solution.py:12
  70.5 8.2 %collective-permute-done.7 = bf16[3,128,512]{2,1,0:T(8,128)(2,1)S(1)} collective-permute-done((bf16[3,128,512]{2,1,0:T(8,128)(2,1)S(1)}, bf16[3,128,512]{2,1,0:T(8,128)(2,1)S(1)}, u32[]{:S(2)}, u32[]{:S(2)}) %collective-permute-start.7) | collective-permute-done | bytes 393248 | tf_op jit(solution)/shard_map/ppermute | solution.py:12
  80.0 2.1 %collective-permute-start.8 = (bf16[3,128,512]{2,1,0:T(8,128)(2,1)S(1)}, bf16[3,128,512]{2,1,0:T(8,128)(2,1)S(1)}, u32[]{:S(2)}, u32[]{:S(2)}) collective-permute-start(bf16[3,128,512]{2,1,0:T(8,128)(2,1)S(1)} %fusion.7), channel_id=1, source_target_pairs={{0,2},{1,3},{2,4},{3,5},{4,6},{5,7},{6,8},{7,9},{8,10},{9,11},{10,... | collective-permute-start | bytes 1179656 | tf_op jit(solution)/shard_map/ppermute | solution.py:12
  82.8 8.6 %collective-permute-done.8 = bf16[3,128,512]{2,1,0:T(8,128)(2,1)S(1)} collective-permute-done((bf16[3,128,512]{2,1,0:T(8,128)(2,1)S(1)}, bf16[3,128,512]{2,1,0:T(8,128)(2,1)S(1)}, u32[]{:S(2)}, u32[]{:S(2)}) %collective-permute-start.8) | collective-permute-done | bytes 393248 | tf_op jit(solution)/shard_map/ppermute | solution.py:12
  92.7 1.9 %collective-permute-start.9 = (bf16[3,128,512]{2,1,0:T(8,128)(2,1)S(1)}, bf16[3,128,512]{2,1,0:T(8,128)(2,1)S(1)}, u32[]{:S(2)}, u32[]{:S(2)}) collective-permute-start(bf16[3,128,512]{2,1,0:T(8,128)(2,1)S(1)} %fusion.8), channel_id=1, source_target_pairs={{0,4},{1,5},{2,6},{3,7},{4,8},{5,9},{6,10},{7,11},{8,12},{9,13},{1... | collective-permute-start | bytes 1179656 | tf_op jit(solution)/shard_map/ppermute | solution.py:12
  95.4 7.9 %collective-permute-done.9 = bf16[3,128,512]{2,1,0:T(8,128)(2,1)S(1)} collective-permute-done((bf16[3,128,512]{2,1,0:T(8,128)(2,1)S(1)}, bf16[3,128,512]{2,1,0:T(8,128)(2,1)S(1)}, u32[]{:S(2)}, u32[]{:S(2)}) %collective-permute-start.9) | collective-permute-done | bytes 393248 | tf_op jit(solution)/shard_map/ppermute | solution.py:12
  104.2 1.1 %fusion.9 = bf16[3,128,512]{2,1,0:T(8,128)(2,1)} fusion(bf16[3,128,512]{2,1,0:T(8,128)(2,1)S(1)} %fusion.8, bf16[10,512,512]{2,1,0:T(8,128)(2,1)S(1)} %bitcast.269, bf16[3,128,1,512]{3,1,2,0:T(8,128)(2,1)S(1)} %fusion.90), kind=kOutput, calls=%fused_computation.28 | convolution fusion | flops 201916416 | bytes 1703936 | tf_op jit(solution)/shard_map/stc,co->sto/dot_general | solution.py:61
  105.3 1.1 %fusion.10 = bf16[3,128,512]{2,1,0:T(8,128)(2,1)} fusion(f32[3,128,512]{2,1,0:T(8,128)S(1)} %convolution_add_fusion.1, bf16[10,512,512]{2,1,0:T(8,128)(2,1)S(1)} %bitcast.244, bf16[3,128,1,512]{3,1,2,0:T(8,128)(2,1)S(1)} %fusion.90), kind=kOutput, calls=%fused_computation.29 | convolution fusion | flops 201719808 | bytes 2097152 | tf_op jit(solution)/shard_map/stc,co->sto/dot_general | solution.py:62
  (63 shorter events, 15.3 us)
Async XLA Ops:
  0.6 14.5 %slice-start.2 = ((s8[5242880]{0:T(1024)(128)(4,1)}), s8[4194304]{0:T(1024)(128)(4,1)S(1)}, s32[]{:S(2)}) async-start(s8[5242880]{0:T(1024)(128)(4,1)} %bitcast.268), calls=%async_computation.2 | async-start | bytes 8388608
  1.5 12.5 %copy-start = (f32[10,2,512]{2,1,0:T(2,128)S(1)}, f32[10,2,512]{2,1,0:T(2,128)}, u32[]{:S(2)}) copy-start(f32[10,2,512]{2,1,0:T(2,128)} %param.6) | copy-start | bytes 122884
  1.6 12.6 %copy-start.1 = (bf16[3,128,512]{2,1,0:T(8,128)(2,1)S(1)}, bf16[3,128,512]{2,1,0:T(8,128)(2,1)}, u32[]{:S(2)}) copy-start(bf16[3,128,512]{2,1,0:T(8,128)(2,1)} %param.5) | copy-start | bytes 1179652
  1.6 13.5 %slice-start.3 = ((s8[5242880]{0:T(1024)(128)(4,1)}), s8[1048576]{0:T(1024)(128)(4,1)S(1)}, s32[]{:S(2)}) async-start(s8[5242880]{0:T(1024)(128)(4,1)} %bitcast.268), calls=%async_computation.3 | async-start | bytes 2097152
  1.6 12.5 %collective-permute-start = (bf16[3,1,512]{2,1,0:T(2,128)(2,1)S(1)}, bf16[3,1,512]{2,1,0:T(2,128)(2,1)S(1)}, u32[]{:S(2)}, u32[]{:S(2)}) collective-permute-start(bf16[3,1,512]{2,1,0:T(2,128)(2,1)S(1)} %slice.253), channel_id=1, source_target_pairs={{0,1},{1,2},{2,3},{3,4},{4,5},{5,6},{6,7},{7,8},{8,9},{9,10},{10,1... | collective-permute-start | bytes 9224 | tf_op jit(solution)/shard_map/ppermute | solution.py:12
  15.5 6.7 %collective-permute-start.1 = (bf16[3,2,512]{2,1,0:T(2,128)(2,1)S(1)}, bf16[3,2,512]{2,1,0:T(2,128)(2,1)S(1)}, u32[]{:S(2)}, u32[]{:S(2)}) collective-permute-start(bf16[3,2,512]{2,1,0:T(2,128)(2,1)S(1)} %slice.338), channel_id=1, source_target_pairs={{0,1},{1,2},{2,3},{3,4},{4,5},{5,6},{6,7},{7,8},{8,9},{9,10},{10,1... | collective-permute-start | bytes 18440 | tf_op jit(solution)/shard_map/ppermute | solution.py:12
  23.6 6.8 %collective-permute-start.2 = (bf16[3,4,512]{2,1,0:T(4,128)(2,1)S(1)}, bf16[3,4,512]{2,1,0:T(4,128)(2,1)S(1)}, u32[]{:S(2)}, u32[]{:S(2)}) collective-permute-start(bf16[3,4,512]{2,1,0:T(4,128)(2,1)S(1)} %slice.342), channel_id=1, source_target_pairs={{0,1},{1,2},{2,3},{3,4},{4,5},{5,6},{6,7},{7,8},{8,9},{9,10},{10,1... | collective-permute-start | bytes 36872 | tf_op jit(solution)/shard_map/ppermute | solution.py:12
  30.4 11.7 %slice-start = ((s8[5242880]{0:T(1024)(128)(4,1)}), s8[4194304]{0:T(1024)(128)(4,1)S(1)}, s32[]{:S(2)}) async-start(s8[5242880]{0:T(1024)(128)(4,1)} %bitcast.243), calls=%async_computation | async-start | bytes 8388608
  31.7 10.3 %slice-start.1 = ((s8[5242880]{0:T(1024)(128)(4,1)}), s8[1048576]{0:T(1024)(128)(4,1)S(1)}, s32[]{:S(2)}) async-start(s8[5242880]{0:T(1024)(128)(4,1)} %bitcast.243), calls=%async_computation.1 | async-start | bytes 2097152
  31.8 7.1 %collective-permute-start.3 = (bf16[3,8,512]{2,1,0:T(8,128)(2,1)S(1)}, bf16[3,8,512]{2,1,0:T(8,128)(2,1)S(1)}, u32[]{:S(2)}, u32[]{:S(2)}) collective-permute-start(bf16[3,8,512]{2,1,0:T(8,128)(2,1)S(1)} %slice.346), channel_id=1, source_target_pairs={{0,1},{1,2},{2,3},{3,4},{4,5},{5,6},{6,7},{7,8},{8,9},{9,10},{10,1... | collective-permute-start | bytes 73736 | tf_op jit(solution)/shard_map/ppermute | solution.py:12
  40.1 7.2 %collective-permute-start.4 = (bf16[3,16,512]{2,1,0:T(8,128)(2,1)S(1)}, bf16[3,16,512]{2,1,0:T(8,128)(2,1)S(1)}, u32[]{:S(2)}, u32[]{:S(2)}) collective-permute-start(bf16[3,16,512]{2,1,0:T(8,128)(2,1)S(1)} %slice.350), channel_id=1, source_target_pairs={{0,1},{1,2},{2,3},{3,4},{4,5},{5,6},{6,7},{7,8},{8,9},{9,10},{10,1... | collective-permute-start | bytes 147464 | tf_op jit(solution)/shard_map/ppermute | solution.py:12
  48.7 7.7 %collective-permute-start.5 = (bf16[3,32,512]{2,1,0:T(8,128)(2,1)S(1)}, bf16[3,32,512]{2,1,0:T(8,128)(2,1)S(1)}, u32[]{:S(2)}, u32[]{:S(2)}) collective-permute-start(bf16[3,32,512]{2,1,0:T(8,128)(2,1)S(1)} %slice.354), channel_id=1, source_target_pairs={{0,1},{1,2},{2,3},{3,4},{4,5},{5,6},{6,7},{7,8},{8,9},{9,10},{10,1... | collective-permute-start | bytes 294920 | tf_op jit(solution)/shard_map/ppermute | solution.py:12
  57.7 8.8 %collective-permute-start.6 = (bf16[3,64,512]{2,1,0:T(8,128)(2,1)S(1)}, bf16[3,64,512]{2,1,0:T(8,128)(2,1)S(1)}, u32[]{:S(2)}, u32[]{:S(2)}) collective-permute-start(bf16[3,64,512]{2,1,0:T(8,128)(2,1)S(1)} %get-tuple-element.12), channel_id=1, source_target_pairs={{0,1},{1,2},{2,3},{3,4},{4,5},{5,6},{6,7},{7,8},{8,9},{9,10},{10,1... | collective-permute-start | bytes 589832 | tf_op jit(solution)/shard_map/ppermute | solution.py:12
  67.8 10.9 %collective-permute-start.7 = (bf16[3,128,512]{2,1,0:T(8,128)(2,1)S(1)}, bf16[3,128,512]{2,1,0:T(8,128)(2,1)S(1)}, u32[]{:S(2)}, u32[]{:S(2)}) collective-permute-start(bf16[3,128,512]{2,1,0:T(8,128)(2,1)S(1)} %fusion.6), channel_id=1, source_target_pairs={{0,1},{1,2},{2,3},{3,4},{4,5},{5,6},{6,7},{7,8},{8,9},{9,10},{10,1... | collective-permute-start | bytes 1179656 | tf_op jit(solution)/shard_map/ppermute | solution.py:12
  80.0 11.5 %collective-permute-start.8 = (bf16[3,128,512]{2,1,0:T(8,128)(2,1)S(1)}, bf16[3,128,512]{2,1,0:T(8,128)(2,1)S(1)}, u32[]{:S(2)}, u32[]{:S(2)}) collective-permute-start(bf16[3,128,512]{2,1,0:T(8,128)(2,1)S(1)} %fusion.7), channel_id=1, source_target_pairs={{0,2},{1,3},{2,4},{3,5},{4,6},{5,7},{6,8},{7,9},{8,10},{9,11},{10,... | collective-permute-start | bytes 1179656 | tf_op jit(solution)/shard_map/ppermute | solution.py:12
  92.7 10.6 %collective-permute-start.9 = (bf16[3,128,512]{2,1,0:T(8,128)(2,1)S(1)}, bf16[3,128,512]{2,1,0:T(8,128)(2,1)S(1)}, u32[]{:S(2)}, u32[]{:S(2)}) collective-permute-start(bf16[3,128,512]{2,1,0:T(8,128)(2,1)S(1)} %fusion.8), channel_id=1, source_target_pairs={{0,4},{1,5},{2,6},{3,7},{4,8},{5,9},{6,10},{7,11},{8,12},{9,13},{1... | collective-permute-start | bytes 1179656 | tf_op jit(solution)/shard_map/ppermute | solution.py:12
where the time goes:
time: 107 us; the launch traced here: 106 us
  waiting for transfers between devices  54.6 us (51%)
  starting transfers between devices  21.2 us (20%)
  matrix products  14.8 us (14%)
  local copies, waits for them, and re-layouts  11.5 us (11%)
  other arithmetic  3.15 us (3%)
  between operations  1.2 us (1%)
    ppermute x10, waiting for transfers between devices, shifted(): lax.ppermute(value, axis, [(source, source + steps) for source in range(l...  54.6 us
    ppermute x10, starting transfers between devices, shifted(): lax.ppermute(value, axis, [(source, source + steps) for source in range(l...  21.2 us
    slice x1, local copies, waits for them, and re-layouts, local(): gate_w = w_gate[layer]  10.4 us
    dot_general x10, matrix products, local(): jnp.einsum('stc,cko->stko', lax.all_gather(conv, 'chan', axis=2, tiled=Tr...  5.91 us
    dot_general x10, matrix products, local(): jnp.einsum('stc,co->sto', piece, res_w, preferred_element_type=jnp.float32)  4.46 us
    dot_general x10, matrix products, local(): jnp.einsum('stc,co->sto', piece, skip_w, preferred_element_type=jnp.float32)  4.41 us
    convert_element_type x10, other arithmetic, gate_units(): (jnp.tanh(hidden[:, :, 0]) * jax.nn.sigmoid(hidden[:, :, 1])).astype(jnp....  3.15 us
  transfers between devices with their start and end apart: 10, of which 9 were waited for; matrix products, arithmetic and copies ran while one was open for 13% of the time, Pallas kernels for 0%

commit v1 on v0

--- a/solution.py
+++ b/solution.py
@@ -1,9 +1,16 @@
+import functools
+
 import jax
 import jax.numpy as jnp
 from jax import lax
+from jax.experimental import pallas as pl
+from jax.experimental.pallas import tpu as pltpu
 from jax.sharding import PartitionSpec as P
 
-LAYERS = 10
+MESH = pl.DeviceIdType.MESH
+BF16, F32 = jnp.bfloat16, jnp.float32
+ALIGN = 16
+VMEM_LIMIT = 60 * 1024 * 1024
 
 
 def shifted(value, axis, steps):
@@ -41,7 +48,7 @@
     stream = signal
     seqs, length, local_c = stream.shape
     skip = jnp.zeros((seqs, length, local_c), jnp.float32)
-    for layer in range(LAYERS):
+    for layer in range(taps.shape[0]):
         delayed = delay_block(stream, 2**layer, near_time, far_time)
         conv = (
             taps[layer, 0] * delayed.astype(jnp.float32)
@@ -65,6 +72,213 @@
     return (stream, skip.astype(jnp.bfloat16))
 
 
+def tanh_gate(filt, gate):
+    return (jnp.tanh(filt) * (0.5 * jnp.tanh(0.5 * gate) + 0.5)).astype(BF16)
+
+
+def kernel(n, layers, near, sig, taps, wg_hbm, wr_hbm, ws_hbm, out_x, out_skip, *scratch):
+    wg, wr, ws, xs, skip, w_sem, send_sem, recv_sem = scratch[:8]
+    halos = scratch[8:]
+    seqs, length, width = sig.shape
+    me = lax.axis_index("tm")
+    clean = near - 1
+    steps = [max(1, 2**layer // length) for layer in range(layers)]
+    reach = sorted(set(steps))
+    rows_of = [min(length, max(ALIGN, 2**layer)) for layer in range(layers)]
+    half = min(256, width)
+
+    def weights(layer):
+        return [
+            pltpu.make_async_copy(wg_hbm.at[layer], wg.at[layer], w_sem.at[layer, 0]),
+            pltpu.make_async_copy(wr_hbm.at[layer], wr.at[layer], w_sem.at[layer, 1]),
+            pltpu.make_async_copy(ws_hbm.at[layer], ws.at[layer], w_sem.at[layer, 2]),
+        ]
+
+    for layer in range(layers):
+        for copy in weights(layer):
+            copy.start()
+
+    barrier = pltpu.get_barrier_semaphore()
+    for step in reach:
+        for ok, other in ((me + step < n, me + step), (me >= step, me - step)):
+
+            @pl.when(ok)
+            def _(other=other):
+                pl.semaphore_signal(barrier, inc=1, device_id={"tm": other}, device_id_type=MESH)
+
+    def source(layer):
+        return sig if layer == 0 else xs.at[layer - 1]
+
+    def send(layer, s):
+        rows = rows_of[layer]
+        return pltpu.make_async_remote_copy(
+            src_ref=source(layer).at[s, pl.ds(length - rows, rows)],
+            dst_ref=halos[layer].at[s],
+            send_sem=send_sem.at[layer, s],
+            recv_sem=recv_sem.at[layer, s],
+            device_id={"tm": me + steps[layer]},
+            device_id_type=MESH,
+        )
+
+    def start_send(layer, which):
+        @pl.when(me + steps[layer] < n)
+        def _():
+            for s in which:
+                send(layer, s).start()
+
+    def take(layer, which):
+        @pl.when(me >= steps[layer])
+        def _():
+            for s in which:
+                send(layer, s).wait_recv()
+
+        @pl.when(me < steps[layer])
+        def _():
+            for s in which:
+                halos[layer][s] = jnp.zeros(halos[layer].shape[1:], BF16)
+
+    def load(layer, s, low, high):
+        return source(layer)[s, low:high]
+
+    def finish(layer, delayed, own, which, low, high, fresh=False):
+        count = high - low
+        own_f = jnp.concatenate(own, axis=0).astype(F32) if len(own) > 1 else own[0].astype(F32)
+        late = jnp.concatenate(delayed, axis=0) if len(delayed) > 1 else delayed[0]
+        conv = (taps[layer, 0:1] * late.astype(F32) + taps[layer, 1:2] * own_f).astype(BF16)
+        parts = []
+        for at in range(0, width, half):
+            filt = jnp.dot(conv, wg[layer, 0, :, at : at + half], preferred_element_type=F32)
+            gate = jnp.dot(conv, wg[layer, 1, :, at : at + half], preferred_element_type=F32)
+            parts.append(tanh_gate(filt, gate))
+        z = jnp.concatenate(parts, axis=1) if len(parts) > 1 else parts[0]
+        last = layer == layers - 1
+        for at in range(0, width, half):
+            cols = slice(at, at + half)
+            update = jnp.dot(z, wr[layer, :, cols], preferred_element_type=F32)
+            new = (own_f[:, cols] + update).astype(BF16)
+            for i, s in enumerate(which):
+                part = new[i * count : (i + 1) * count]
+                if last:
+                    out_x[s, low:high, cols] = part
+                else:
+                    xs[layer, s, low:high, cols] = part
+        if not last:
+            yield
+        for at in range(0, width, half):
+            cols = slice(at, at + half)
+            more = jnp.dot(z, ws[layer, :, cols], preferred_element_type=F32)
+            for i, s in enumerate(which):
+                part = more[i * count : (i + 1) * count]
+                if not fresh:
+                    part = skip[s, low:high, cols] + part
+                if last:
+                    out_skip[s, low:high, cols] = part.astype(BF16)
+                else:
+                    skip[s, low:high, cols] = part
+        if last:
+            yield
+
+    every = list(range(seqs))
+    top = [max(ALIGN, 2 ** (layer + 1)) for layer in range(clean)]
+    first = [0 if 2 ** (layer + 2) <= ALIGN * 1 else 0 for layer in range(clean)]
+    for layer in range(clean - 1, -1, -1):
+        need = top[layer] if layer == clean - 1 else first[layer + 1] - 2 ** (layer + 1)
+        first[layer] = max(0, min(need, top[layer]) // ALIGN * ALIGN)
+
+    for layer in range(clean):
+        delay, low = 2**layer, first[layer]
+        for copy in weights(layer):
+            copy.wait()
+        delayed, own = [], []
+        for s in every:
+            if delay < ALIGN:
+                begin = max(0, low - ALIGN)
+                block = pltpu.roll(load(layer, s, begin, length).astype(F32), delay, 0)
+                delayed.append(block[low - begin :])
+            else:
+                delayed.append(load(layer, s, low - delay, length - delay))
+            own.append(load(layer, s, low, length))
+        work = finish(layer, delayed, own, every, low, length, fresh=layer == 0)
+        next(work)
+        if layer == 0:
+            total = sum(((me + step < n).astype(jnp.int32) + (me >= step).astype(jnp.int32)) for step in reach)
+            pl.semaphore_wait(barrier, total)
+            start_send(0, every)
+        start_send(layer + 1, every)
+        for _ in work:
+            pass
+
+    for layer in range(clean):
+        delay, high = 2**layer, top[layer]
+        take(layer, every)
+        delayed, own = [], []
+        for s in every:
+            rows = rows_of[layer]
+            tail = halos[layer][s]
+            if delay < ALIGN:
+                joined = jnp.concatenate([tail.astype(F32), load(layer, s, 0, high).astype(F32)], axis=0)
+                delayed.append(pltpu.roll(joined, delay, 0)[rows:])
+            else:
+                delayed.append(jnp.concatenate([tail, load(layer, s, 0, high - delay)], axis=0))
+            own.append(load(layer, s, 0, high))
+        for _ in finish(layer, delayed, own, every, 0, high, fresh=layer == 0):
+            pass
+
+    for layer in range(clean, layers):
+        for copy in weights(layer):
+            copy.wait()
+        for s in every:
+            take(layer, [s])
+            late = halos[layer][s]
+            if 2**layer < length:
+                late = jnp.concatenate([late, load(layer, s, 0, length - 2**layer)], axis=0)
+            work = finish(layer, [late], [load(layer, s, 0, length)], [s], 0, length)
+            next(work)
+            if layer + 1 < layers:
+                start_send(layer + 1, [s])
+            for _ in work:
+                pass
+
+    for layer in range(layers):
+
+        @pl.when(me + steps[layer] < n)
+        def _(layer=layer):
+            for s in every:
+                send(layer, s).wait_send()
+
+
+def fused(n, signal, taps, w_gate, w_res, w_skip):
+    seqs, length, width = signal.shape
+    layers = taps.shape[0]
+    near = length.bit_length() - 1
+    halves = jnp.transpose(w_gate, (0, 2, 1, 3))
+    halos = [
+        pltpu.VMEM((seqs, min(length, max(ALIGN, 2**layer)), width), BF16) for layer in range(layers)
+    ]
+    flops = 2 * seqs * length * width * width * 4 * layers
+    in_vmem, anywhere = pl.BlockSpec(memory_space=pltpu.VMEM), pl.BlockSpec(memory_space=pl.ANY)
+    return pl.pallas_call(
+        functools.partial(kernel, n, layers, near),
+        out_shape=[jax.ShapeDtypeStruct(signal.shape, BF16)] * 2,
+        in_specs=[in_vmem, in_vmem, anywhere, anywhere, anywhere],
+        out_specs=[in_vmem, in_vmem],
+        scratch_shapes=[
+            pltpu.VMEM((layers, 2, width, width), BF16),
+            pltpu.VMEM((layers, width, width), BF16),
+            pltpu.VMEM((layers, width, width), BF16),
+            pltpu.VMEM((layers - 1, seqs, length, width), BF16),
+            pltpu.VMEM((seqs, length, width), F32),
+            pltpu.SemaphoreType.DMA((layers, 3)),
+            pltpu.SemaphoreType.DMA((layers, seqs)),
+            pltpu.SemaphoreType.DMA((layers, seqs)),
+            *halos,
+        ],
+        compiler_params=pltpu.CompilerParams(collective_id=0, has_side_effects=True, vmem_limit_bytes=VMEM_LIMIT),
+        cost_estimate=pl.CostEstimate(flops=flops, bytes_accessed=8 * layers * width * width, transcendentals=0),
+        name="stack",
+    )(signal, taps, halves, w_res, w_skip)
+
+
 def solution(mesh):
     in_specs = (
         P(None, "tm", "chan"),
@@ -74,4 +288,12 @@
         P(None, None, "chan"),
     )
     out_specs = (P(None, "tm", "chan"), P(None, "tm", "chan"))
-    return jax.shard_map(local, mesh=mesh, in_specs=in_specs, out_specs=out_specs, check_vma=False)
+
+    def body(*args):
+        length, layers = args[0].shape[1], args[1].shape[0]
+        power = length & (length - 1) == 0 and length >= 4 * ALIGN and 2 ** (layers - 1) >= length
+        if mesh.shape["chan"] == 1 and power:
+            return tuple(fused(mesh.shape["tm"], *args))
+        return local(*args)
+
+    return jax.shard_map(body, mesh=mesh, in_specs=in_specs, out_specs=out_specs, check_vma=False)

time: 107 us -> 52.7 us (0.49)
  the two profiles are of different devices: /device:TPU:8 before, /device:TPU:11 now
where the time goes in v1:
time: 52.7 us; the launch traced here: 52.5 us
  Pallas kernels  38.2 us (72%)
  local copies, waits for them, and re-layouts  13.7 us (26%)
  between operations  0.64 us (1%)
    pallas_call x1, Pallas kernels, fused(): pl.pallas_call(functools.partial(kernel, n, layers, near), out_shape=[jax...  38.2 us
    unnamed x3, local copies, waits for them, and re-layouts  13.7 us

profile of v1, /device:TPU:11, one launch (start us, length us, event | category | flops | bytes accessed | tf_op | source)
XLA Modules:
  0.0 52.5 jit_solution(11080557202319263978)
XLA Ops:
  0.6 10.1 %copy.9 = bf16[10,512,2,512]{3,1,2,0:T(8,128)(2,1)} copy(bf16[10,512,2,512]{3,2,1,0:T(2,128)(2,1)} %param.7) | data formatting | bytes 20971520 | tf_op args[2]
  10.8 38.2 %stack.1 = (bf16[3,128,512]{2,1,0:T(8,128)(2,1)}, bf16[3,128,512]{2,1,0:T(8,128)(2,1)}) custom-call(bf16[3,128,512]{2,1,0:T(8,128)(2,1)} %sig.1, f32[10,2,512]{2,1,0:T(2,128)} %taps.1, bf16[10,2,512,512]{3,2,1,0:T(8,128)(2,1)} %bitcast.3, bf16[10,512,512]{2,1,0:T(8,128)(2,1)} %wr_hbm.1, bf16[10,512,512]{2,1,0:T(8,128)(2,1)} %ws_hbm.1), custom_call_target="tpu_custom_call" | custom-call | flops 8053063680 | bytes 20971520 | tf_op jit(solution)/shard_map/stack/pallas_call | solution.py:260
  48.9 1.8 %copy.12 = bf16[3,128,512]{2,1,0:T(8,128)(2,1)} copy(bf16[3,128,512]{2,1,0:T(8,128)(2,1)} %get-tuple-element.4) | data formatting | bytes 786432
  50.7 1.8 %copy.13 = bf16[3,128,512]{2,1,0:T(8,128)(2,1)} copy(bf16[3,128,512]{2,1,0:T(8,128)(2,1)} %get-tuple-element.5) | data formatting | bytes 786432

commit v2 on v1

--- a/solution.py
+++ b/solution.py
@@ -10,7 +10,7 @@
 MESH = pl.DeviceIdType.MESH
 BF16, F32 = jnp.bfloat16, jnp.float32
 ALIGN = 16
-VMEM_LIMIT = 60 * 1024 * 1024
+VMEM_LIMIT = 56000 * 1024
 
 
 def shifted(value, axis, steps):
@@ -76,9 +76,23 @@
     return (jnp.tanh(filt) * (0.5 * jnp.tanh(0.5 * gate) + 0.5)).astype(BF16)
 
 
-def kernel(n, layers, near, sig, taps, wg_hbm, wr_hbm, ws_hbm, out_x, out_skip, *scratch):
-    wg, wr, ws, xs, skip, w_sem, send_sem, recv_sem = scratch[:8]
-    halos = scratch[8:]
+def split_pairs(pairs, out):
+    width = pairs.shape[0]
+    block = min(128, width)
+    row = lax.broadcasted_iota(jnp.int32, (2 * block, 2 * block), 0)
+    column = lax.broadcasted_iota(jnp.int32, (2 * block, 2 * block), 1)
+    wanted = jnp.where(row < block, 2 * row, 2 * (row - block) + 1)
+    order = jnp.where(column == wanted, 1.0, 0.0).astype(F32).astype(BF16)
+    for at in range(0, width, block):
+        both = pairs[at : at + block].reshape(2 * block, pairs.shape[2])
+        sorted_rows = jnp.dot(order, both, preferred_element_type=F32).astype(BF16)
+        out[0, at : at + block] = sorted_rows[:block]
+        out[1, at : at + block] = sorted_rows[block:]
+
+
+def kernel(n, layers, near, sig_hbm, taps_hbm, wg_hbm, wr_hbm, ws_hbm, out_x, out_skip, *scratch):
+    sig, taps, raw, wg, wr, ws, xs, skip, in_sem, w_sem, send_sem, recv_sem = scratch[:12]
+    halos = scratch[12:]
     seqs, length, width = sig.shape
     me = lax.axis_index("tm")
     clean = near - 1
@@ -89,11 +103,17 @@
 
     def weights(layer):
         return [
-            pltpu.make_async_copy(wg_hbm.at[layer], wg.at[layer], w_sem.at[layer, 0]),
+            pltpu.make_async_copy(wg_hbm.at[layer], raw.at[layer], w_sem.at[layer, 0]),
             pltpu.make_async_copy(wr_hbm.at[layer], wr.at[layer], w_sem.at[layer, 1]),
             pltpu.make_async_copy(ws_hbm.at[layer], ws.at[layer], w_sem.at[layer, 2]),
         ]
 
+    inputs = [
+        pltpu.make_async_copy(sig_hbm, sig, in_sem.at[0]),
+        pltpu.make_async_copy(taps_hbm, taps, in_sem.at[1]),
+    ]
+    for copy in inputs:
+        copy.start()
     for layer in range(layers):
         for copy in weights(layer):
             copy.start()
@@ -185,10 +205,13 @@
         need = top[layer] if layer == clean - 1 else first[layer + 1] - 2 ** (layer + 1)
         first[layer] = max(0, min(need, top[layer]) // ALIGN * ALIGN)
 
+    for copy in inputs:
+        copy.wait()
     for layer in range(clean):
         delay, low = 2**layer, first[layer]
         for copy in weights(layer):
             copy.wait()
+        split_pairs(raw.at[layer], wg.at[layer])
         delayed, own = [], []
         for s in every:
             if delay < ALIGN:
@@ -208,6 +231,13 @@
         for _ in work:
             pass
 
+    def arrive(layer):
+        for copy in weights(layer):
+            copy.wait()
+        split_pairs(raw.at[layer], wg.at[layer])
+
+    arrive(clean)
+
     for layer in range(clean):
         delay, high = 2**layer, top[layer]
         take(layer, every)
@@ -225,8 +255,9 @@
             pass
 
     for layer in range(clean, layers):
-        for copy in weights(layer):
-            copy.wait()
+        if layer == clean + 1:
+            for later in range(layer, layers):
+                arrive(later)
         for s in every:
             take(layer, [s])
             late = halos[layer][s]
@@ -251,7 +282,6 @@
     seqs, length, width = signal.shape
     layers = taps.shape[0]
     near = length.bit_length() - 1
-    halves = jnp.transpose(w_gate, (0, 2, 1, 3))
     halos = [
         pltpu.VMEM((seqs, min(length, max(ALIGN, 2**layer)), width), BF16) for layer in range(layers)
     ]
@@ -259,15 +289,19 @@
     in_vmem, anywhere = pl.BlockSpec(memory_space=pltpu.VMEM), pl.BlockSpec(memory_space=pl.ANY)
     return pl.pallas_call(
         functools.partial(kernel, n, layers, near),
-        out_shape=[jax.ShapeDtypeStruct(signal.shape, BF16)] * 2,
-        in_specs=[in_vmem, in_vmem, anywhere, anywhere, anywhere],
+        out_shape=[pltpu.VMEM(signal.shape, BF16)] * 2,
+        in_specs=[anywhere] * 5,
         out_specs=[in_vmem, in_vmem],
         scratch_shapes=[
+            pltpu.VMEM(signal.shape, BF16),
+            pltpu.VMEM(taps.shape, F32),
+            pltpu.VMEM((layers, width, 2, width), BF16),
             pltpu.VMEM((layers, 2, width, width), BF16),
             pltpu.VMEM((layers, width, width), BF16),
             pltpu.VMEM((layers, width, width), BF16),
             pltpu.VMEM((layers - 1, seqs, length, width), BF16),
             pltpu.VMEM((seqs, length, width), F32),
+            pltpu.SemaphoreType.DMA((2,)),
             pltpu.SemaphoreType.DMA((layers, 3)),
             pltpu.SemaphoreType.DMA((layers, seqs)),
             pltpu.SemaphoreType.DMA((layers, seqs)),
@@ -276,7 +310,7 @@
         compiler_params=pltpu.CompilerParams(collective_id=0, has_side_effects=True, vmem_limit_bytes=VMEM_LIMIT),
         cost_estimate=pl.CostEstimate(flops=flops, bytes_accessed=8 * layers * width * width, transcendentals=0),
         name="stack",
-    )(signal, taps, halves, w_res, w_skip)
+    )(signal, taps, w_gate, w_res, w_skip)
 
 
 def solution(mesh):

time: 52.7 us -> 46 us (0.87)
  the two profiles are of different devices: /device:TPU:11 before, /device:TPU:8 now
where the time goes in v2:
time: 46 us; the launch traced here: 45.6 us
  Pallas kernels  43.5 us (95%)
  local copies, waits for them, and re-layouts  1.49 us (3%)
  between operations  0.64 us (1%)
    pallas_call x1, Pallas kernels, fused(): pl.pallas_call(functools.partial(kernel, n, layers, near), out_shape=[plt...  43.5 us
    unnamed x2, local copies, waits for them, and re-layouts  1.49 us

profile of v2, /device:TPU:8, one launch (start us, length us, event | category | flops | bytes accessed | tf_op | source)
XLA Modules:
  0.0 45.6 jit_solution(9399806560325680243)
XLA Ops:
  0.6 43.5 %stack.1 = (bf16[3,128,512]{2,1,0:T(8,128)(2,1)S(1)}, bf16[3,128,512]{2,1,0:T(8,128)(2,1)S(1)}) custom-call(bf16[3,128,512]{2,1,0:T(8,128)(2,1)} %sig_hbm.1, f32[10,2,512]{2,1,0:T(2,128)} %taps_hbm.1, bf16[10,512,2,512]{3,2,1,0:T(2,128)(2,1)} %wg_hbm.1, bf16[10,512,512]{2,1,0:T(8,128)(2,1)} %wr_hbm.1, bf16[10,512,512]{2,1,0:T(8,128)(2,1)} %ws_hbm.1), custom_call_target="tpu_custom_call" | custom-call | flops 8053063680 | bytes 20971520 | tf_op jit(solution)/shard_map/stack/pallas_call | solution.py:290
  44.1 0.7 %copy.9 = bf16[3,128,512]{2,1,0:T(8,128)(2,1)} copy(bf16[3,128,512]{2,1,0:T(8,128)(2,1)S(1)} %get-tuple-element.2) | data formatting | bytes 786432
  44.9 0.7 %copy.10 = bf16[3,128,512]{2,1,0:T(8,128)(2,1)} copy(bf16[3,128,512]{2,1,0:T(8,128)(2,1)S(1)} %get-tuple-element.3) | data formatting | bytes 786432

commit v3 on v2

--- a/solution.py
+++ b/solution.py
@@ -91,11 +91,12 @@
 
 
 def kernel(n, layers, near, sig_hbm, taps_hbm, wg_hbm, wr_hbm, ws_hbm, out_x, out_skip, *scratch):
-    sig, taps, raw, wg, wr, ws, xs, skip, in_sem, w_sem, send_sem, recv_sem = scratch[:12]
-    halos = scratch[12:]
+    sig, taps, raw, wg, wr, ws, xs, zs, skip, in_sem, w_sem, send_sem, recv_sem = scratch[:13]
+    halos = scratch[13:]
     seqs, length, width = sig.shape
     me = lax.axis_index("tm")
     clean = near - 1
+    held = zs.shape[0]
     steps = [max(1, 2**layer // length) for layer in range(layers)]
     reach = sorted(set(steps))
     rows_of = [min(length, max(ALIGN, 2**layer)) for layer in range(layers)]
@@ -160,7 +161,7 @@
     def load(layer, s, low, high):
         return source(layer)[s, low:high]
 
-    def finish(layer, delayed, own, which, low, high, fresh=False):
+    def finish(layer, delayed, own, which, low, high):
         count = high - low
         own_f = jnp.concatenate(own, axis=0).astype(F32) if len(own) > 1 else own[0].astype(F32)
         late = jnp.concatenate(delayed, axis=0) if len(delayed) > 1 else delayed[0]
@@ -172,6 +173,9 @@
             parts.append(tanh_gate(filt, gate))
         z = jnp.concatenate(parts, axis=1) if len(parts) > 1 else parts[0]
         last = layer == layers - 1
+        if layer < held:
+            for i, s in enumerate(which):
+                zs[layer, s, low:high] = z[i * count : (i + 1) * count]
         for at in range(0, width, half):
             cols = slice(at, at + half)
             update = jnp.dot(z, wr[layer, :, cols], preferred_element_type=F32)
@@ -184,13 +188,14 @@
                     xs[layer, s, low:high, cols] = part
         if not last:
             yield
+        if layer < held:
+            return
         for at in range(0, width, half):
             cols = slice(at, at + half)
             more = jnp.dot(z, ws[layer, :, cols], preferred_element_type=F32)
             for i, s in enumerate(which):
                 part = more[i * count : (i + 1) * count]
-                if not fresh:
-                    part = skip[s, low:high, cols] + part
+                part = skip[s, low:high, cols] + part
                 if last:
                     out_skip[s, low:high, cols] = part.astype(BF16)
                 else:
@@ -221,7 +226,7 @@
             else:
                 delayed.append(load(layer, s, low - delay, length - delay))
             own.append(load(layer, s, low, length))
-        work = finish(layer, delayed, own, every, low, length, fresh=layer == 0)
+        work = finish(layer, delayed, own, every, low, length)
         next(work)
         if layer == 0:
             total = sum(((me + step < n).astype(jnp.int32) + (me >= step).astype(jnp.int32)) for step in reach)
@@ -251,7 +256,7 @@
             else:
                 delayed.append(jnp.concatenate([tail, load(layer, s, 0, high - delay)], axis=0))
             own.append(load(layer, s, 0, high))
-        for _ in finish(layer, delayed, own, every, 0, high, fresh=layer == 0):
+        for _ in finish(layer, delayed, own, every, 0, high):
             pass
 
     for layer in range(clean, layers):
@@ -269,6 +274,14 @@
                 start_send(layer + 1, [s])
             for _ in work:
                 pass
+        if layer == held - 1:
+            for at in range(0, width, half):
+                total = None
+                for before in range(held):
+                    gated = zs[before].reshape(seqs * length, width)
+                    more = jnp.dot(gated, ws[before, :, at : at + half], preferred_element_type=F32)
+                    total = more if total is None else total + more
+                skip[:, :, at : at + half] = total.reshape(seqs, length, half)
 
     for layer in range(layers):
 
@@ -282,6 +295,7 @@
     seqs, length, width = signal.shape
     layers = taps.shape[0]
     near = length.bit_length() - 1
+    held = min(near + 1, layers - 1)
     halos = [
         pltpu.VMEM((seqs, min(length, max(ALIGN, 2**layer)), width), BF16) for layer in range(layers)
     ]
@@ -300,6 +314,7 @@
             pltpu.VMEM((layers, width, width), BF16),
             pltpu.VMEM((layers, width, width), BF16),
             pltpu.VMEM((layers - 1, seqs, length, width), BF16),
+            pltpu.VMEM((held, seqs, length, width), BF16),
             pltpu.VMEM((seqs, length, width), F32),
             pltpu.SemaphoreType.DMA((2,)),
             pltpu.SemaphoreType.DMA((layers, 3)),

time: 46 us -> 44.6 us (0.970)
  Pallas kernels: 43.5 us -> 42.1 us
    pallas_call x1, Pallas kernels: 43.5 us -> 42.1 us  [fused(): pl.pallas_call(functools.partial(kernel, n, layers, near), out_shape=[plt...]
where the time goes in v3:
time: 44.6 us; the launch traced here: 44.2 us
  Pallas kernels  42.1 us (94%)
  local copies, waits for them, and re-layouts  1.49 us (3%)
  between operations  0.64 us (1%)
    pallas_call x1, Pallas kernels, fused(): pl.pallas_call(functools.partial(kernel, n, layers, near), out_shape=[plt...  42.1 us
    unnamed x2, local copies, waits for them, and re-layouts  1.49 us

profile of v3, /device:TPU:8, one launch (start us, length us, event | category | flops | bytes accessed | tf_op | source)
XLA Modules:
  0.0 44.2 jit_solution(14474602183893549184)
XLA Ops:
  0.6 42.1 %stack.1 = (bf16[3,128,512]{2,1,0:T(8,128)(2,1)S(1)}, bf16[3,128,512]{2,1,0:T(8,128)(2,1)S(1)}) custom-call(bf16[3,128,512]{2,1,0:T(8,128)(2,1)} %sig_hbm.1, f32[10,2,512]{2,1,0:T(2,128)} %taps_hbm.1, bf16[10,512,2,512]{3,2,1,0:T(2,128)(2,1)} %wg_hbm.1, bf16[10,512,512]{2,1,0:T(8,128)(2,1)} %wr_hbm.1, bf16[10,512,512]{2,1,0:T(8,128)(2,1)} %ws_hbm.1), custom_call_target="tpu_custom_call" | custom-call | flops 8053063680 | bytes 20971520 | tf_op jit(solution)/shard_map/stack/pallas_call | solution.py:304
  42.7 0.7 %copy.9 = bf16[3,128,512]{2,1,0:T(8,128)(2,1)} copy(bf16[3,128,512]{2,1,0:T(8,128)(2,1)S(1)} %get-tuple-element.2) | data formatting | bytes 786432
  43.5 0.7 %copy.10 = bf16[3,128,512]{2,1,0:T(8,128)(2,1)} copy(bf16[3,128,512]{2,1,0:T(8,128)(2,1)S(1)} %get-tuple-element.3) | data formatting | bytes 786432
